TPU v7x, 32 devices: a whole 2x2x4 slice. The times are simulated.
32 devices in a mesh: space: 32 (over z, y, x, core), mem: 1.
Axes of the slice: x: 2, y: 2, z: 4, core: 2. Of those that a mesh axis runs over, the one named last changes fastest.
Arguments:
- members: bfloat16 [128, 768, 2, 384], P(('space', 'mem')), may hold values from -6 to 6
- state: float32 [768, 2, 384], P('space'), may hold values from -6 to 6
- cotangent: float32 [768, 2, 384], P('space'), may hold values from -6 to 6
- conv_in: float32 [3, 3, 128, 2], replicated, may hold values from -1.5 to 1.5
- conv_out: float32 [3, 3, 2, 128], replicated, may hold values from -0.1875 to 0.1875
- bias: float32 [128], replicated, may hold values from -3 to 3
Outputs:
- increment: float32 [768, 2, 384], P('space')
- response: float32 [768, 2, 384], P('space')
All inputs are finite; a program needn't handle non-finite values.
Results may differ from a plain program's by a relative error of at most 0.0045.
Values may be sent and summed in bfloat16 or wider, within the bound.
A program may use at most 64 MiB of HBM per device.

v0:
```python
import functools

import jax
import jax.numpy as jnp
from jax import lax
from jax.experimental import pallas as pl
from jax.experimental.pallas import tpu as pltpu
from jax.sharding import PartitionSpec as P

HALF = 16


def flip(index, stride):
    return index + stride * (1 - 2 * lax.rem(index // stride, 2))


def flip_all(index, mask):
    stride = 1
    while stride <= mask:
        if mask & stride:
            index = flip(index, stride)
        stride *= 2
    return index


def stages_of(count):
    held = [0]
    steps = []
    stride = count // 2
    while stride >= 8:
        steps.append([(stride, list(held))])
        held = held + [m ^ stride for m in held]
        stride //= 2
    half = max(1, len(held) // 2)
    first, second = held[:half], held[half:]
    steps.append([(2, first), (4, second)])
    first = first + [m ^ 2 for m in first]
    second = second + [m ^ 4 for m in second]
    steps.append([(4, first), (2, second)])
    return steps


def greet(me, count, extra=()):
    barrier = pltpu.get_barrier_semaphore()
    friends = list(extra)
    stride = 1
    while stride < count:
        friends.append(flip(me, stride))
        stride *= 2
    for friend in friends:
        pl.semaphore_signal(
            barrier, inc=1, device_id={"space": friend}, device_id_type=pl.DeviceIdType.MESH
        )
    pl.semaphore_wait(barrier, len(friends))


def gather_kernel(count, block_ref, whole_ref, send_sem, recv_sem):
    me = lax.axis_index("space")
    greet(me, count)

    def remote(mask, stride):
        owner = flip_all(me, mask)
        source = block_ref if mask == 0 else whole_ref.at[owner]
        slot = mask ^ stride
        return pltpu.make_async_remote_copy(
            src_ref=source,
            dst_ref=whole_ref.at[owner],
            send_sem=send_sem.at[slot],
            recv_sem=recv_sem.at[slot],
            device_id={"space": flip(me, stride)},
            device_id_type=pl.DeviceIdType.MESH,
        )

    started = []
    pair = []
    for step in stages_of(count):
        now = []
        for position in range(max(len(masks) for stride, masks in step)):
            for stride, masks in step:
                if position < len(masks):
                    copy = remote(masks[position], stride)
                    copy.start()
                    now.append((copy, masks[position] ^ stride))
        if not pair:
            copy = remote(0, 1)
            copy.start()
            pair.append(copy)
            whole_ref[me] = block_ref[...]
        for copy, mask in now:
            copy.wait_recv()
            other = remote(mask, 1)
            other.start()
            pair.append(other)
            started.append(copy)
    for copy in started:
        copy.wait_send()
    for copy in pair:
        copy.wait()


def gather(block):
    count = lax.axis_size("space")
    return pl.pallas_call(
        functools.partial(gather_kernel, count),
        out_shape=jax.ShapeDtypeStruct((count,) + block.shape, block.dtype),
        in_specs=[pl.BlockSpec(memory_space=pltpu.VMEM)],
        out_specs=pl.BlockSpec(memory_space=pltpu.VMEM),
        scratch_shapes=[
            pltpu.SemaphoreType.DMA((count,)),
            pltpu.SemaphoreType.DMA((count,)),
        ],
        compiler_params=pltpu.CompilerParams(collective_id=0, has_side_effects=True),
        name="gather",
    )(block)


def scatter_kernel(
    count, rim, part_ref, sum_ref, left_ref, right_ref,
    out_buf, in_buf, edge_buf, send_sem, recv_sem, edge_send, edge_recv,
):
    me = lax.axis_index("space")
    before, after = lax.rem(me + count - 1, count), lax.rem(me + 1, count)
    greet(me, count, (before, after))
    arrived = {mask: [] for mask in range(count)}

    def value(mask):
        total = part_ref[flip_all(me, mask)]
        for slot in arrived[mask]:
            total = total + in_buf[slot].astype(jnp.float32)
        return total

    sent = []
    for step in [[(1, list(range(0, count, 2)))]] + stages_of(count)[::-1]:
        now = []
        for position in range(max(len(masks) for stride, masks in step)):
            for stride, masks in step:
                if position < len(masks):
                    slot = masks[position] ^ stride
                    out_buf[slot] = value(slot).astype(out_buf.dtype)
                    copy = pltpu.make_async_remote_copy(
                        src_ref=out_buf.at[slot],
                        dst_ref=in_buf.at[slot],
                        send_sem=send_sem.at[slot],
                        recv_sem=recv_sem.at[slot],
                        device_id={"space": flip(me, stride)},
                        device_id_type=pl.DeviceIdType.MESH,
                    )
                    copy.start()
                    now.append((copy, masks[position], slot))
        for copy, mask, slot in now:
            copy.wait_recv()
            arrived[mask].append(slot)
            sent.append(copy)
    total = value(0)
    sum_ref[...] = total
    edge_buf[0] = total[:rim]
    edge_buf[1] = total[total.shape[0] - rim :]
    edges = [
        pltpu.make_async_remote_copy(
            src_ref=edge_buf.at[side],
            dst_ref=target,
            send_sem=edge_send.at[side],
            recv_sem=edge_recv.at[side],
            device_id={"space": friend},
            device_id_type=pl.DeviceIdType.MESH,
        )
        for side, target, friend in ((0, right_ref, before), (1, left_ref, after))
    ]
    for copy in edges:
        copy.start()
    for copy in sent:
        copy.wait_send()
    for copy in edges:
        copy.wait()


def scatter(parts, rim):
    count, rows, lat_count = parts.shape
    return pl.pallas_call(
        functools.partial(scatter_kernel, count, rim),
        out_shape=(
            jax.ShapeDtypeStruct((rows, lat_count), jnp.float32),
            jax.ShapeDtypeStruct((rim, lat_count), jnp.float32),
            jax.ShapeDtypeStruct((rim, lat_count), jnp.float32),
        ),
        in_specs=[pl.BlockSpec(memory_space=pltpu.VMEM)],
        out_specs=(pl.BlockSpec(memory_space=pltpu.VMEM),) * 3,
        scratch_shapes=[
            pltpu.VMEM((count, rows, lat_count), jnp.bfloat16),
            pltpu.VMEM((count, rows, lat_count), jnp.bfloat16),
            pltpu.VMEM((2, rim, lat_count), jnp.float32),
            pltpu.SemaphoreType.DMA((count,)),
            pltpu.SemaphoreType.DMA((count,)),
            pltpu.SemaphoreType.DMA((2,)),
            pltpu.SemaphoreType.DMA((2,)),
        ],
        compiler_params=pltpu.CompilerParams(collective_id=1, has_side_effects=True),
        name="scatter",
    )(parts)


def padded_2(cells, axis, width):
    count = lax.axis_size(axis)
    head = cells[:width]
    tail = cells[cells.shape[0] - width :]
    return jnp.concatenate(
        [
            lax.ppermute(tail, axis, [(i, (i + 1) % count) for i in range(count)]),
            cells,
            lax.ppermute(head, axis, [((i + 1) % count, i) for i in range(count)]),
        ],
        axis=0,
    )


def convolve(padded, weight):
    row_count = padded.shape[0] - 2
    lat_count = padded.shape[2]
    out_count = weight.shape[2]
    in_count = weight.shape[3]
    padded = padded.astype(jnp.bfloat16)
    weight = weight.astype(jnp.bfloat16)
    if out_count <= in_count:
        flattened = weight.reshape(9 * out_count, in_count)
        product = jnp.einsum(
            "kc,xcy->xky", flattened, padded, preferred_element_type=jnp.float32
        )
        product = jnp.pad(product, ((0, 0), (0, 0), (1, 1)))
        summed = jnp.zeros((row_count, out_count, lat_count), jnp.float32)
        for step_lon in range(3):
            for step_lat in range(3):
                tap_index = step_lon * 3 + step_lat
                summed = (
                    summed
                    + product[
                        step_lon : step_lon + row_count,
                        tap_index * out_count : (tap_index + 1) * out_count,
                        step_lat : step_lat + lat_count,
                    ]
                )
        return summed
    lat_padded = jnp.pad(padded, ((0, 0), (0, 0), (1, 1)))
    stacked = jnp.concatenate(
        [
            lat_padded[step_lon : step_lon + row_count, :, step_lat : step_lat + lat_count]
            for step_lon in range(3)
            for step_lat in range(3)
        ],
        axis=1,
    )
    flattened = jnp.transpose(weight, (2, 0, 1, 3)).reshape(out_count, 9 * in_count)
    return jnp.einsum("ok,xky->xoy", flattened, stacked, preferred_element_type=jnp.float32)


def split(values):
    high = lax.reduce_precision(values, 8, 7)
    return high.astype(jnp.bfloat16), (values - high).astype(jnp.bfloat16)


def convolve_fine(padded, weight):
    out_count, in_count = weight.shape[2:]
    upper, lower = split(padded)
    weight_upper, weight_lower = split(weight)
    if out_count <= in_count:
        both = jnp.concatenate([upper, lower], axis=1)
        stacked = jnp.concatenate([weight_upper, weight_lower], axis=2)
        stacked = jnp.concatenate([stacked, stacked], axis=3)
        result = convolve(both, stacked)
        return result[:, :out_count] + result[:, out_count:]
    return convolve(
        jnp.concatenate([upper, lower, upper], axis=1),
        jnp.concatenate([weight_upper, weight_upper, weight_lower], axis=3),
    )


def flipped(weight):
    return jnp.transpose(weight[::-1, ::-1], (0, 1, 3, 2))


def band_matrix(count, wrap):
    row_index = jnp.arange(count)[:, None]
    col_index = jnp.arange(count)[None, :]
    distance = jnp.abs(row_index - col_index)
    if wrap:
        distance = jnp.minimum(distance, count - distance)
    ratio = distance.astype(jnp.float32) / (HALF + 1.0)
    return jnp.where(distance <= HALF, 1.0 - ratio * ratio, 0.0).astype(jnp.bfloat16)


def per_device(members, state, cotangent, conv_in, conv_out, bias):
    row_count, var_count, lat_count = state.shape
    count = lax.axis_size("space")
    direct = count >= 8 and count & (count - 1) == 0
    rim_width = 2
    joined = jnp.concatenate([state, cotangent], axis=1)
    padded = padded_2(joined, "space", rim_width)
    state_pad = padded[:, :var_count]
    cot_pad = padded[:, var_count:]
    activity = jnp.tanh(convolve_fine(state_pad, conv_in) + bias[None, :, None])
    slopes = 1.0 - activity * activity
    backward = slopes * convolve_fine(cot_pad, flipped(conv_out))
    gradient = cotangent + convolve_fine(backward, flipped(conv_in))
    gradient = gradient.astype(jnp.bfloat16)
    if direct:
        flat = gradient.reshape(row_count * var_count, lat_count)
        whole = gather(flat).reshape(count * row_count, var_count, lat_count)
    else:
        whole = lax.all_gather(gradient, "space", axis=0, tiled=True)
    lat_loc = band_matrix(lat_count, False)
    product = (members.astype(jnp.float32) * whole.astype(jnp.float32)[None]).astype(jnp.bfloat16)
    banded = jnp.einsum(
        "mxcy,yz->mxcz", product, lat_loc, preferred_element_type=jnp.float32
    ).astype(jnp.bfloat16)
    lon_loc = band_matrix(banded.shape[1], True)
    spread = jnp.einsum("zx,mxcy->mzcy", lon_loc, banded, preferred_element_type=jnp.float32)
    contrib = jnp.sum(members.astype(jnp.float32) * spread, axis=0)
    member_count = members.shape[0] * lax.axis_size("space") * lax.axis_size("mem")
    if direct:
        own, left, right = scatter(
            contrib.reshape(count, row_count * var_count, lat_count), rim_width * var_count
        )
        total = jnp.concatenate([left, own, right], axis=0)
        total = total.reshape(row_count + 2 * rim_width, var_count, lat_count)
        if lax.axis_size("mem") > 1:
            total = lax.psum(total, "mem")
        incr_pad = total / (member_count - 1.0)
        increment = incr_pad[rim_width : rim_width + row_count]
    else:
        member_sum = lax.psum(contrib, "mem")
        block_sum = lax.psum_scatter(member_sum, "space", scatter_dimension=0, tiled=True)
        increment = block_sum / (member_count - 1.0)
        incr_pad = padded_2(increment, "space", rim_width)
    tangent_hidden = slopes * convolve(incr_pad, conv_in)
    response = increment + convolve(tangent_hidden, conv_out)
    return (increment, response)


def solution(mesh):
    in_specs = (
        P(("space", "mem"), None, None, None),
        P("space", None, None),
        P("space", None, None),
        P(),
        P(),
        P(),
    )
    out_specs = (P("space", None, None), P("space", None, None))
    return jax.shard_map(
        per_device, mesh=mesh, in_specs=in_specs, out_specs=out_specs, check_vma=False
    )
```

profile of v0, /device:TPU:0, one launch (start us, length us, event | category | flops | bytes accessed | tf_op | source)
XLA Modules:
  0.0 121.7 jit_solution(8179888475635528836)
XLA Ops:
  0.6 0.8 pad_maximum_fusion.4
  1.4 0.5 collective-permute-start
  1.9 6.0 %collective-permute-start.1 = (f32[2,4,384]{2,1,0:T(4,128)S(1)}, f32[2,4,384]{2,1,0:T(4,128)S(1)}, u32[]{:S(2)}, u32[]{:S(2)}) collective-permute-start(f32[2,4,384]{2,1,0:T(4,128)S(1)} %get-tuple-element.33), channel_id=1, source_target_pairs={{1,0},{2,1},{3,2},{4,3},{5,4},{6,5},{7,6},{8,7},{9,8},{10,9},{11,1... | collective-permute-start | bytes 36872 | tf_op jit(solution)/shard_map/ppermute | solution.py:210
  7.9 0.8 convert_bitcast_fusion
  8.7 0.7 reduce-precision_convert_fusion.3
  9.4 0.7 reduce-precision_convert_fusion.4
  10.2 0.7 convert_element_type.121
  11.0 0.0 copy-start
  11.0 0.0 copy-start.1
  11.0 12.4 %copy.10 = bf16[4,768,2,384]{1,3,2,0:T(8,128)(2,1)} copy(bf16[4,768,2,384]{3,2,1,0:T(2,128)(2,1)} %param.6) | data formatting | bytes 9437184 | tf_op args[0]
  23.4 0.0 collective-permute-done
  23.4 0.0 collective-permute-done.1
  23.5 0.0 copy-done
  23.5 0.0 copy-done.1
  23.5 0.1 pad_maximum_fusion
  23.6 0.1 fusion.59
  23.7 0.3 pad_maximum_fusion.1
  24.0 1.2 pad_slice_fusion.18
  25.1 0.3 pad_slice_fusion.12
  25.5 7.9 %concatenate.42 = bf16[26,54,384]{2,1,0:T(8,128)(2,1)S(1)} concatenate(bf16[26,6,384]{2,1,0:T(8,128)(2,1)} %get-tuple-element.31, bf16[26,6,384]{2,1,0:T(8,128)(2,1)} %get-tuple-element.30, bf16[26,6,384]{2,1,0:T(8,128)(2,1)S(1)} %get-tuple-element.24, bf16[26,6,384]{2,1,0:T(8,128)(2,1)S(1)} %get-tuple-element.25, bf16[26,6,384]{2,1,0:T(8,128)(2,1)} %get-tuple-element.29, ...), dimensions={1} | concatenate | bytes 2156544 | tf_op jit(solution)/shard_map/concatenate | solution.py:243
  33.3 3.1 %fusion.87 = f32[26,384,128]{1,2,0:T(8,128)} fusion(bf16[26,54,384]{2,1,0:T(8,128)(2,1)S(1)} %concatenate.42, bf16[128,54,1]{0,1,2:T(8,128)(2,1)S(1)} %reshape.50), kind=kOutput, calls=%fused_computation.124 | convolution fusion | flops 138018816 | bytes 6203904 | tf_op jit(solution)/shard_map/ok,xky->xoy/dot_general | solution.py:252
  36.5 0.0 copy-start.3
  36.5 3.1 %concatenate.45 = bf16[26,54,384]{2,1,0:T(8,128)(2,1)S(1)} concatenate(bf16[26,6,384]{2,1,0:T(8,128)(2,1)S(1)} %get-tuple-element.18, bf16[26,6,384]{2,1,0:T(8,128)(2,1)S(1)} %get-tuple-element.17, bf16[26,6,384]{2,1,0:T(8,128)(2,1)S(1)} %get-tuple-element.11, bf16[26,6,384]{2,1,0:T(8,128)(2,1)S(1)} %get-tuple-element.12, bf16[26,6,384]{2,1,0:T(8,128)(2,1)S(1)} %get-tuple-element.16, ...), dimensions={1} | concatenate | bytes 2156544 | tf_op jit(solution)/shard_map/concatenate | solution.py:243
  39.6 0.0 copy-done.3
  39.6 4.1 %reduce-precision_convert_fusion = (bf16[26,128,384]{2,1,0:T(8,128)(2,1)S(1)}, bf16[26,128,384]{2,1,0:T(8,128)(2,1)S(1)}) fusion(bf16[26,54,384]{2,1,0:T(8,128)(2,1)S(1)} %concatenate.45, bf16[128,54,1]{0,1,2:T(8,128)(2,1)S(1)} %reshape.51, f32[26,384,128]{1,2,0:T(8,128)} %fusion.87, f32[128]{0:T(128)S(1)} %copy-done.3), kind=kOutput, calls=%fused_computation.5 | convolution fusion | flops 148242432 | bytes 11316224 | tf_op jit(solution)/shard_map/ok,xky->xoy/dot_general | solution.py:252
  43.8 1.1 fusion.25
  44.9 0.5 fusion.57
  45.4 0.1 fusion.70
  45.5 0.6 reshape.45.block_ref
  46.1 19.1 %gather.1 = bf16[32,48,384]{2,1,0:T(8,128)(2,1)} custom-call(bf16[48,384]{1,0:T(8,128)(2,1)} %reshape.45.block_ref), custom_call_target="tpu_custom_call" | custom-call | tf_op jit(solution)/shard_map/gather/pallas_call | solution.py:103
  65.3 2.9 %reshape.49 = f32[768,2,384]{2,1,0:T(2,128)S(1)} reshape(bf16[32,48,384]{2,1,0:T(8,128)(2,1)} %gather.1) | data formatting | bytes 3538944 | tf_op jit(solution)/shard_map/convert_element_type | solution.py:310
  68.1 3.6 %copy.11 = f32[768,2,384]{0,2,1:T(8,128)} copy(f32[768,2,384]{2,1,0:T(2,128)S(1)} %reshape.49) | data formatting | bytes 4718592 | tf_op jit(solution)/shard_map/convert_element_type | solution.py:310
  71.7 11.6 %fusion.1 = f32[768,2,384]{0,2,1:T(8,128)} fusion(bf16[4,768,2,384]{1,3,2,0:T(8,128)(2,1)} %copy.10, f32[768,2,384]{0,2,1:T(8,128)} %copy.11), kind=kOutput, calls=%fused_computation.3 | convolution fusion | flops 5459558400 | bytes 9437184 | tf_op jit(solution)/shard_map/zx,mxcy->mzcy/dot_general | solution.py:315
  83.4 3.9 %copy.12 = f32[768,2,384]{2,1,0:T(2,128)S(1)} copy(f32[768,2,384]{0,2,1:T(8,128)} %fusion.1) | data formatting | bytes 4718592 | tf_op jit(solution)/shard_map/reduce_sum | solution.py:316
  87.3 2.9 %reshape.46.part_ref = f32[32,48,384]{2,1,0:T(8,128)} reshape(f32[768,2,384]{2,1,0:T(2,128)S(1)} %copy.12) | data formatting | bytes 4718592 | tf_op jit(solution)/shard_map/reshape | solution.py:320
  90.1 24.1 %scatter.1 = (f32[48,384]{1,0:T(8,128)}, f32[4,384]{1,0:T(4,128)}, f32[4,384]{1,0:T(4,128)}) custom-call(f32[32,48,384]{2,1,0:T(8,128)} %reshape.46.part_ref), custom_call_target="tpu_custom_call" | custom-call | tf_op jit(solution)/shard_map/scatter/pallas_call | solution.py:179
  114.3 0.9 fusion.85
  115.2 0.3 pad_slice_fusion.24
  115.8 0.0 copy-start.2
  115.8 0.8 concatenate.51
  116.6 3.9 %fusion.28 = f32[26,18,384]{2,1,0:T(8,128)S(1)} fusion(bf16[18,128,1]{1,0,2:T(8,128)(2,1)S(1)} %reshape.56, f32[26,384,128]{1,2,0:T(8,128)} %fusion.87, f32[128]{0:T(128)S(1)} %copy-done.3, bf16[26,18,384]{2,1,0:T(8,128)(2,1)S(1)} %concatenate.51, bf16[128,18,1]{0,1,2:T(8,128)(2,1)S(1)} %reshape.55), kind=kOutput, calls=%fused_computation.37 | convolution fusion | flops 98402304 | bytes 6199808 | tf_op jit(solution)/shard_map/kc,xcy->xky/dot_general | solution.py:225
  120.5 0.0 copy-done.2
  120.5 1.2 fusion.66
  (15 shorter events, 0.4 us)
Async XLA Ops:
  1.4 22.0 %collective-permute-start = (f32[2,4,384]{2,1,0:T(4,128)S(1)}, f32[2,4,384]{2,1,0:T(4,128)S(1)}, u32[]{:S(2)}, u32[]{:S(2)}) collective-permute-start(f32[2,4,384]{2,1,0:T(4,128)S(1)} %get-tuple-element.32), channel_id=1, source_target_pairs={{0,1},{1,2},{2,3},{3,4},{4,5},{5,6},{6,7},{7,8},{8,9},{9,10},{10,1... | collective-permute-start | bytes 36872 | tf_op jit(solution)/shard_map/ppermute | solution.py:208
  1.9 21.5 %collective-permute-start.1 = (f32[2,4,384]{2,1,0:T(4,128)S(1)}, f32[2,4,384]{2,1,0:T(4,128)S(1)}, u32[]{:S(2)}, u32[]{:S(2)}) collective-permute-start(f32[2,4,384]{2,1,0:T(4,128)S(1)} %get-tuple-element.33), channel_id=1, source_target_pairs={{1,0},{2,1},{3,2},{4,3},{5,4},{6,5},{7,6},{8,7},{9,8},{10,9},{11,1... | collective-permute-start | bytes 36872 | tf_op jit(solution)/shard_map/ppermute | solution.py:210
  11.0 12.5 %copy-start = (f32[24,2,384]{2,1,0:T(2,128)S(1)}, f32[24,2,384]{2,1,0:T(2,128)}, u32[]{:S(2)}) copy-start(f32[24,2,384]{2,1,0:T(2,128)} %param.8) | copy-start | bytes 221188
  11.0 12.5 %copy-start.1 = (f32[24,2,384]{2,1,0:T(2,128)S(1)}, f32[24,2,384]{2,1,0:T(2,128)}, u32[]{:S(2)}) copy-start(f32[24,2,384]{2,1,0:T(2,128)} %param.7) | copy-start | bytes 221188
  36.5 3.1 %copy-start.3 = (f32[128]{0:T(128)S(1)}, f32[128]{0:T(128)}, u32[]{:S(2)}) copy-start(f32[128]{0:T(128)} %param.11) | copy-start | bytes 1540
  115.8 4.7 %copy-start.2 = (f32[24,2,384]{2,1,0:T(2,128)}, f32[24,2,384]{2,1,0:T(2,128)S(1)}, u32[]{:S(2)}) copy-start(f32[24,2,384]{2,1,0:T(2,128)S(1)} %slice.217) | copy-start | bytes 221188
where the time goes:
time: 123 us; the launch traced here: 122 us
  Pallas kernels  43.3 us (35%)
  local copies, waits for them, and re-layouts  40.2 us (33%)
  matrix products  23.9 us (19%)
  other arithmetic  6.88 us (6%)
  starting transfers between devices  6.52 us (5%)
    pallas_call x1, Pallas kernels, scatter(): pl.pallas_call(functools.partial(scatter_kernel, count, rim), out_shape=(...  24.1 us
    pallas_call x1, Pallas kernels, gather(): pl.pallas_call(functools.partial(gather_kernel, count), out_shape=jax.Sha...  19.1 us
    unnamed x9, local copies, waits for them, and re-layouts  12.4 us
    concatenate x3, local copies, waits for them, and re-layouts, convolve(): jnp.concatenate([lat_padded[step_lon:step_lon + row_count, :, step_lat:st...  11.8 us
    dot_general x1, matrix products, per_device(): jnp.einsum('zx,mxcy->mzcy', lon_loc, banded, preferred_element_type=jnp.f...  11.6 us
    dot_general x2, matrix products, convolve(): jnp.einsum('ok,xky->xoy', flattened, stacked, preferred_element_type=jnp....  7.25 us
    convert_element_type x2, local copies, waits for them, and re-layouts, per_device(): whole.astype(jnp.float32)[None]  6.47 us
    ppermute x1, starting transfers between devices, padded_2(): lax.ppermute(head, axis, [((i + 1) % count, i) for i in range(count)])  5.97 us
  transfers between devices with their start and end apart: 2, of which 0 were waited for; matrix products, arithmetic and copies ran while one was open for 13% of the time, Pallas kernels for 0%

commit v1 on v0

--- a/solution.py
+++ b/solution.py
@@ -199,6 +199,47 @@
     )(parts)
 
 
+def covariance_kernel(members_ref, whole_ref, lat_ref, lon_ref, sum_ref, banded_ref):
+    lat_count = lat_ref.shape[0]
+
+    @pl.when(pl.program_id(0) == 0)
+    def _():
+        sum_ref[...] = jnp.zeros_like(sum_ref)
+
+    for start in range(0, whole_ref.shape[1], lat_count):
+        columns = slice(start, start + lat_count)
+        product = members_ref[0, :, columns].astype(jnp.float32) * whole_ref[:, columns].astype(
+            jnp.float32
+        )
+        banded_ref[:, columns] = jnp.dot(
+            product.astype(jnp.bfloat16), lat_ref[...], preferred_element_type=jnp.float32
+        ).astype(jnp.bfloat16)
+    for start in range(0, whole_ref.shape[1], lat_count):
+        columns = slice(start, start + lat_count)
+        spread = jnp.dot(
+            lon_ref[...], banded_ref[:, columns], preferred_element_type=jnp.float32
+        )
+        sum_ref[:, columns] += members_ref[0, :, columns].astype(jnp.float32) * spread
+
+
+def covariance(members, whole, lat_loc, lon_loc):
+    count, lon_count, width = members.shape
+    return pl.pallas_call(
+        covariance_kernel,
+        grid=(count,),
+        out_shape=jax.ShapeDtypeStruct((lon_count, width), jnp.float32),
+        in_specs=[
+            pl.BlockSpec((1, lon_count, width), lambda m: (m, 0, 0)),
+            pl.BlockSpec(whole.shape, lambda m: (0, 0)),
+            pl.BlockSpec(lat_loc.shape, lambda m: (0, 0)),
+            pl.BlockSpec(lon_loc.shape, lambda m: (0, 0)),
+        ],
+        out_specs=pl.BlockSpec((lon_count, width), lambda m: (0, 0)),
+        scratch_shapes=[pltpu.VMEM((lon_count, width), jnp.bfloat16)],
+        name="covariance",
+    )(members, whole, lat_loc, lon_loc)
+
+
 def padded_2(cells, axis, width):
     count = lax.axis_size(axis)
     head = cells[:width]
@@ -213,13 +254,14 @@
     )
 
 
-def convolve(padded, weight):
+def convolve(padded, weight, precision=None):
     row_count = padded.shape[0] - 2
     lat_count = padded.shape[2]
     out_count = weight.shape[2]
     in_count = weight.shape[3]
-    padded = padded.astype(jnp.bfloat16)
-    weight = weight.astype(jnp.bfloat16)
+    if precision is None:
+        padded = padded.astype(jnp.bfloat16)
+        weight = weight.astype(jnp.bfloat16)
     if out_count <= in_count:
         flattened = weight.reshape(9 * out_count, in_count)
         product = jnp.einsum(
@@ -249,7 +291,9 @@
         axis=1,
     )
     flattened = jnp.transpose(weight, (2, 0, 1, 3)).reshape(out_count, 9 * in_count)
-    return jnp.einsum("ok,xky->xoy", flattened, stacked, preferred_element_type=jnp.float32)
+    return jnp.einsum(
+        "ok,xky->xoy", flattened, stacked, precision=precision, preferred_element_type=jnp.float32
+    )
 
 
 def split(values):
@@ -267,10 +311,7 @@
         stacked = jnp.concatenate([stacked, stacked], axis=3)
         result = convolve(both, stacked)
         return result[:, :out_count] + result[:, out_count:]
-    return convolve(
-        jnp.concatenate([upper, lower, upper], axis=1),
-        jnp.concatenate([weight_upper, weight_upper, weight_lower], axis=3),
-    )
+    return convolve(padded, weight, lax.Precision.HIGH)
 
 
 def flipped(weight):
@@ -301,23 +342,20 @@
     backward = slopes * convolve_fine(cot_pad, flipped(conv_out))
     gradient = cotangent + convolve_fine(backward, flipped(conv_in))
     gradient = gradient.astype(jnp.bfloat16)
+    width = var_count * lat_count
+    gradient = gradient.reshape(row_count, width)
     if direct:
-        flat = gradient.reshape(row_count * var_count, lat_count)
-        whole = gather(flat).reshape(count * row_count, var_count, lat_count)
+        whole = gather(gradient).reshape(count * row_count, width)
     else:
         whole = lax.all_gather(gradient, "space", axis=0, tiled=True)
+    merged = members.reshape(members.shape[0], members.shape[1], width)
     lat_loc = band_matrix(lat_count, False)
-    product = (members.astype(jnp.float32) * whole.astype(jnp.float32)[None]).astype(jnp.bfloat16)
-    banded = jnp.einsum(
-        "mxcy,yz->mxcz", product, lat_loc, preferred_element_type=jnp.float32
-    ).astype(jnp.bfloat16)
-    lon_loc = band_matrix(banded.shape[1], True)
-    spread = jnp.einsum("zx,mxcy->mzcy", lon_loc, banded, preferred_element_type=jnp.float32)
-    contrib = jnp.sum(members.astype(jnp.float32) * spread, axis=0)
+    lon_loc = band_matrix(merged.shape[1], True)
+    contrib = covariance(merged, whole, lat_loc, lon_loc)
     member_count = members.shape[0] * lax.axis_size("space") * lax.axis_size("mem")
     if direct:
         own, left, right = scatter(
-            contrib.reshape(count, row_count * var_count, lat_count), rim_width * var_count
+            contrib.reshape(count, row_count, width), rim_width
         )
         total = jnp.concatenate([left, own, right], axis=0)
         total = total.reshape(row_count + 2 * rim_width, var_count, lat_count)
@@ -328,7 +366,7 @@
     else:
         member_sum = lax.psum(contrib, "mem")
         block_sum = lax.psum_scatter(member_sum, "space", scatter_dimension=0, tiled=True)
-        increment = block_sum / (member_count - 1.0)
+        increment = block_sum.reshape(state.shape) / (member_count - 1.0)
         incr_pad = padded_2(increment, "space", rim_width)
     tangent_hidden = slopes * convolve(incr_pad, conv_in)
     response = increment + convolve(tangent_hidden, conv_out)

time: 123 us -> 105 us (0.85)
  local copies, waits for them, and re-layouts: 40.2 us -> 17 us
  Pallas kernels: 43.3 us -> 55.6 us
  matrix products: 23.9 us -> 15.6 us
  other arithmetic: 6.88 us -> 8.45 us
    pallas_call x0 -> x1, Pallas kernels: none -> 12.3 us  [covariance(): pl.pallas_call(covariance_kernel, grid=(count,), out_shape=jax.ShapeDtype...]
    unnamed x9, local copies, waits for them, and re-layouts: 12.4 us -> 0.65 us
    concatenate x3, local copies, waits for them, and re-layouts: 11.8 us -> 2.32 us  [convolve(): jnp.concatenate([lat_padded[step_lon:step_lon + row_count, :, step_lat:st...]
    dot_general x3 -> x2, matrix products: 18.9 us -> 10.5 us  [convolve(): jnp.einsum('ok,xky->xoy', flattened, stacked, precision=precision, prefer...]
    reshape x2 -> x1, local copies, waits for them, and re-layouts: 3.5 us -> 11.4 us  [per_device(): merged = members.reshape(members.shape[0], members.shape[1], width)]
    convert_element_type x2 -> x0, local copies, waits for them, and re-layouts: 6.47 us -> none  [per_device(): whole.astype(jnp.float32)[None]]
    reduce_sum x1 -> x0, local copies, waits for them, and re-layouts: 3.89 us -> none  [per_device(): contrib = jnp.sum(members.astype(jnp.float32) * spread, axis=0)]
    convert_element_type x0 -> x2, other arithmetic: none -> 2.62 us  [band_matrix(): jnp.where(distance <= HALF, 1.0 - ratio * ratio, 0.0).astype(jnp.bfloat16)]
  transfers between devices with their start and end apart: 2 -> 2, of which waited for: 0 -> 0; matrix products, arithmetic and copies ran while one was open for 13% -> 16% of each run, Pallas kernels for 0% -> 0%
where the time goes in v1:
time: 105 us; the launch traced here: 104 us
  Pallas kernels  55.6 us (53%)
  local copies, waits for them, and re-layouts  17 us (16%)
  matrix products  15.6 us (15%)
  other arithmetic  8.45 us (8%)
  starting transfers between devices  6.52 us (6%)
    pallas_call x1, Pallas kernels, scatter(): pl.pallas_call(functools.partial(scatter_kernel, count, rim), out_shape=(...  24.1 us
    pallas_call x1, Pallas kernels, gather(): pl.pallas_call(functools.partial(gather_kernel, count), out_shape=jax.Sha...  19.2 us
    pallas_call x1, Pallas kernels, covariance(): pl.pallas_call(covariance_kernel, grid=(count,), out_shape=jax.ShapeDtype...  12.3 us
    reshape x1, local copies, waits for them, and re-layouts, per_device(): merged = members.reshape(members.shape[0], members.shape[1], width)  11.4 us
    dot_general x2, matrix products, convolve(): jnp.einsum('ok,xky->xoy', flattened, stacked, precision=precision, prefer...  10.5 us
    ppermute x1, starting transfers between devices, padded_2(): lax.ppermute(head, axis, [((i + 1) % count, i) for i in range(count)])  5.97 us
    dot_general x2, matrix products, convolve(): jnp.einsum('kc,xcy->xky', flattened, padded, preferred_element_type=jnp.f...  5.03 us
    convert_element_type x2, other arithmetic, band_matrix(): jnp.where(distance <= HALF, 1.0 - ratio * ratio, 0.0).astype(jnp.bfloat16)  2.62 us
  transfers between devices with their start and end apart: 2, of which 0 were waited for; matrix products, arithmetic and copies ran while one was open for 16% of the time, Pallas kernels for 0%

profile of v1, /device:TPU:0, one launch (start us, length us, event | category | flops | bytes accessed | tf_op | source)
XLA Modules:
  0.0 104.1 jit_solution(17729614231557913497)
XLA Ops:
  0.6 0.8 pad_maximum_fusion.3
  1.4 0.5 collective-permute-start
  1.9 6.0 %collective-permute-start.1 = (f32[2,4,384]{2,1,0:T(4,128)S(1)}, f32[2,4,384]{2,1,0:T(4,128)S(1)}, u32[]{:S(2)}, u32[]{:S(2)}) collective-permute-start(f32[2,4,384]{2,1,0:T(4,128)S(1)} %get-tuple-element.21), channel_id=1, source_target_pairs={{1,0},{2,1},{3,2},{4,3},{5,4},{6,5},{7,6},{8,7},{9,8},{10,9},{11,1... | collective-permute-start | bytes 36872 | tf_op jit(solution)/shard_map/ppermute | solution.py:251
  7.9 1.8 %select_convert_fusion.lon_ref = bf16[768,768]{1,0:T(8,128)(2,1)} fusion(), kind=kLoop, calls=%fused_computation.20 | loop fusion | flops 6488064 | bytes 1179648 | tf_op jit(solution)/shard_map/convert_element_type | solution.py:328
  9.7 0.8 select_convert_fusion.1.lat_ref
  10.5 0.7 reduce-precision_convert_fusion.1
  11.2 0.7 convert_bitcast_fusion
  11.9 0.8 fusion.47
  12.7 0.7 reshape.49
  13.5 0.0 copy-start
  13.5 0.0 copy-start.1
  13.5 11.4 %reshape.40.members_ref = bf16[4,768,768]{2,1,0:T(8,128)(2,1)} reshape(bf16[4,768,2,384]{3,2,1,0:T(2,128)(2,1)} %param.6) | data formatting | bytes 9437184 | tf_op jit(solution)/shard_map/reshape | solution.py:351
  25.0 0.0 collective-permute-done
  25.0 0.0 collective-permute-done.1
  25.0 0.0 copy-done
  25.0 0.0 copy-done.1
  25.0 0.1 pad_maximum_fusion
  25.1 0.1 fusion.43
  25.2 0.1 fusion.42
  25.2 1.1 %pad_slice_fusion.12 = (f32[26,2,384]{2,1,0:T(2,128)S(1)}, f32[26,2,384]{2,1,0:T(2,128)S(1)}, f32[26,2,384]{2,1,0:T(2,128)S(1)}, f32[26,2,384]{2,1,0:T(2,128)S(1...) fusion(f32[28,2,384]{2,1,0:T(2,128)S(1)} %get-tuple-element.12,, ...), kind=kLoop, calls=%fused_computation.57 | loop fusion | bytes 1130496 | tf_op jit(solution)/shard_map/slice | solution.py:287
  26.3 0.1 pad_maximum_fusion.1
  26.4 0.1 fusion.44
  26.5 0.8 concatenate.39
  27.3 0.0 copy-start.3
  27.3 4.5 %fusion.48 = f32[26,384,128]{1,2,0:T(8,128)} fusion(f32[26,18,384]{2,1,0:T(8,128)S(1)} %concatenate.39, f32[128,18,1]{0,1,2:T(8,128)S(1)} %reshape.49), kind=kOutput, calls=%fused_computation.92 | convolution fusion | flops 138018816 | bytes 5839872 | tf_op jit(solution)/shard_map/ok,xky->xoy/dot_general | solution.py:294
  31.8 0.8 concatenate.40
  32.5 0.0 copy-done.3
  32.5 6.1 %reduce-precision_convert_fusion = (bf16[26,128,384]{2,1,0:T(8,128)(2,1)S(1)}, bf16[26,128,384]{2,1,0:T(8,128)(2,1)S(1)}) fusion(f32[26,18,384]{2,1,0:T(8,128)S(1)} %concatenate.40, f32[128,18,1]{0,1,2:T(8,128)S(1)} %reshape.50, f32[26,384,128]{1,2,0:T(8,128)} %fusion.48, f32[128]{0:T(128)S(1)} %copy-done.3), kind=kOutput, calls=%fused_computation.1 | convolution fusion | flops 148242432 | bytes 10952192 | tf_op jit(solution)/shard_map/ok,xky->xoy/dot_general | solution.py:294
  38.6 1.1 %fusion.12 = f32[26,36,384]{2,1,0:T(8,128)S(1)} fusion(bf16[36,256,1]{1,0,2:T(8,128)(2,1)S(1)} %reshape.51, bf16[26,128,384]{2,1,0:T(8,128)(2,1)S(1)} %get-tuple-element.9, bf16[26,128,384]{2,1,0:T(8,128)(2,1)S(1)} %get-tuple-element.8), kind=kOutput, calls=%fused_computation.28 | convolution fusion | flops 194248704 | bytes 6567936 | tf_op jit(solution)/shard_map/kc,xcy->xky/dot_general | solution.py:267
  39.8 0.5 fusion.26
  40.3 0.1 fusion.37
  40.4 0.6 copy.8
  41.0 19.2 %gather.1 = bf16[32,24,768]{2,1,0:T(8,128)(2,1)} custom-call(bf16[24,768]{1,0:T(8,128)(2,1)} %bitcast.40), custom_call_target="tpu_custom_call" | custom-call | tf_op jit(solution)/shard_map/gather/pallas_call | solution.py:103
  60.2 12.3 %covariance.1 = f32[768,768]{1,0:T(8,128)} custom-call(bf16[4,768,768]{2,1,0:T(8,128)(2,1)} %reshape.40.members_ref, bf16[768,768]{1,0:T(8,128)(2,1)} %bitcast.39, bf16[384,384]{1,0:T(8,128)(2,1)} %select_convert_fusion.1.lat_ref, bf16[768,768]{1,0:T(8,128)(2,1)} %select_convert_fusion.lon_ref), custom_call_target="tpu_custom_call" | custom-call | tf_op jit(solution)/shard_map/covariance/pallas_call | solution.py:227
  72.5 24.1 %scatter.1 = (f32[24,768]{1,0:T(8,128)}, f32[2,768]{1,0:T(2,128)}, f32[2,768]{1,0:T(2,128)}) custom-call(f32[32,24,768]{2,1,0:T(8,128)} %bitcast.38), custom_call_target="tpu_custom_call" | custom-call | tf_op jit(solution)/shard_map/scatter/pallas_call | solution.py:179
  96.6 0.9 fusion.41
  97.6 0.3 pad_slice_fusion.24
  98.2 0.0 copy-start.2
  98.2 0.8 concatenate.45
  99.0 3.9 %fusion.15 = f32[26,18,384]{2,1,0:T(8,128)S(1)} fusion(bf16[18,128,1]{1,0,2:T(8,128)(2,1)S(1)} %reshape.53, f32[26,384,128]{1,2,0:T(8,128)} %fusion.48, f32[128]{0:T(128)S(1)} %copy-done.3, bf16[26,18,384]{2,1,0:T(8,128)(2,1)S(1)} %concatenate.45, bf16[128,18,1]{0,1,2:T(8,128)(2,1)S(1)} %reshape.52), kind=kOutput, calls=%fused_computation.29 | convolution fusion | flops 98402304 | bytes 6199808 | tf_op jit(solution)/shard_map/kc,xcy->xky/dot_general | solution.py:267
  102.9 0.0 copy-done.2
  102.9 1.2 %fusion.33 = f32[24,2,384]{2,1,0:T(2,128)} fusion(f32[24,2,384]{2,1,0:T(2,128)S(1)} %slice.227, f32[26,18,384]{2,1,0:T(8,128)S(1)} %fusion.15), kind=kLoop, calls=%fused_computation.51 | loop fusion | flops 165888 | bytes 1327104 | tf_op jit(solution)/shard_map/add | solution.py:372
  (12 shorter events, 0.3 us)
Async XLA Ops:
  1.4 23.6 %collective-permute-start = (f32[2,4,384]{2,1,0:T(4,128)S(1)}, f32[2,4,384]{2,1,0:T(4,128)S(1)}, u32[]{:S(2)}, u32[]{:S(2)}) collective-permute-start(f32[2,4,384]{2,1,0:T(4,128)S(1)} %get-tuple-element.20), channel_id=1, source_target_pairs={{0,1},{1,2},{2,3},{3,4},{4,5},{5,6},{6,7},{7,8},{8,9},{9,10},{10,1... | collective-permute-start | bytes 36872 | tf_op jit(solution)/shard_map/ppermute | solution.py:249
  1.9 23.0 %collective-permute-start.1 = (f32[2,4,384]{2,1,0:T(4,128)S(1)}, f32[2,4,384]{2,1,0:T(4,128)S(1)}, u32[]{:S(2)}, u32[]{:S(2)}) collective-permute-start(f32[2,4,384]{2,1,0:T(4,128)S(1)} %get-tuple-element.21), channel_id=1, source_target_pairs={{1,0},{2,1},{3,2},{4,3},{5,4},{6,5},{7,6},{8,7},{9,8},{10,9},{11,1... | collective-permute-start | bytes 36872 | tf_op jit(solution)/shard_map/ppermute | solution.py:251
  13.5 11.5 %copy-start = (f32[24,2,384]{2,1,0:T(2,128)S(1)}, f32[24,2,384]{2,1,0:T(2,128)}, u32[]{:S(2)}) copy-start(f32[24,2,384]{2,1,0:T(2,128)} %param.8) | copy-start | bytes 221188
  13.5 11.5 %copy-start.1 = (f32[24,2,384]{2,1,0:T(2,128)S(1)}, f32[24,2,384]{2,1,0:T(2,128)}, u32[]{:S(2)}) copy-start(f32[24,2,384]{2,1,0:T(2,128)} %param.7) | copy-start | bytes 221188
  27.3 5.2 %copy-start.3 = (f32[128]{0:T(128)S(1)}, f32[128]{0:T(128)}, u32[]{:S(2)}) copy-start(f32[128]{0:T(128)} %param.11) | copy-start | bytes 1540
  98.2 4.7 %copy-start.2 = (f32[24,2,384]{2,1,0:T(2,128)}, f32[24,2,384]{2,1,0:T(2,128)S(1)}, u32[]{:S(2)}) copy-start(f32[24,2,384]{2,1,0:T(2,128)S(1)} %slice.227) | copy-start | bytes 221188
